TPU v7x, 32 devices: a 4x4x1 block of a 4x4x8 slice. The times are simulated.
32 devices in a mesh: dp: 2 (over z, core), tp: 16 (over x, y).
Axes of the slice: x: 4, y: 4, z: 1, core: 2. Of those that a mesh axis runs over, the one named last changes fastest.
The devices are a block of a 4x4x8 slice.
Arguments:
- x: bfloat16 [3072, 12288], P(('dp', 'tp')), parts along dimension 0
- w_gate: bfloat16 [12288, 28672], P(None, 'tp')
- w_up: bfloat16 [12288, 28672], P(None, 'tp')
- w_down: bfloat16 [28672, 12288], P('tp')
Outputs:
- output: bfloat16 [3072, 12288], P(('dp', 'tp')), parts along dimension 0
There are 2 independent parts. A program takes and returns all parts, laid end to end along the dimension named above; an argument that names none is the same for every part.
All inputs are finite; a program needn't handle non-finite values.
Results may differ from a plain program's by a relative error of at most 0.016.
Values are sent between devices in bfloat16 or wider.
A program may use at most 768 MiB of HBM per device.

v0:
```python
import jax
import jax.numpy as jnp
from jax import lax
from jax.sharding import PartitionSpec as P


def solution(mesh):
    def step(x, w_gate, w_up, w_down):
        rows = lax.all_gather(x, "tp", axis=0, tiled=True)
        gate = jnp.dot(rows, w_gate, preferred_element_type=jnp.float32)
        up = jnp.dot(rows, w_up, preferred_element_type=jnp.float32)
        hidden = (jax.nn.silu(gate) * up).astype(jnp.bfloat16)
        term = jnp.dot(hidden, w_down, preferred_element_type=jnp.float32).astype(jnp.bfloat16)
        return lax.psum_scatter(term, "tp", scatter_dimension=0, tiled=True)

    return jax.shard_map(
        step,
        mesh=mesh,
        in_specs=(P(("dp", "tp"), None), P(None, "tp"), P(None, "tp"), P("tp", None)),
        out_specs=P(("dp", "tp"), None),
        check_vma=False,
    )
```

profile of v0, /device:TPU:97, one launch (start us, length us, event | category | flops | bytes accessed | tf_op | source)
XLA Modules:
  0.0 679.7 jit_solution(17880314494011633935)
XLA Ops:
  6.5 0.0 all-gather.2.cloned.1.call-start
  6.6 0.7 all-gather.2.cloned.1.call-update
  7.3 0.1 reduce-scatter.2.cloned.1.call-start
  7.4 218.9 %all-gather.2.cloned.1.call-done = bf16[1536,12288]{1,0:T(8,128)(2,1)} async-done(((bf16[96,12288]{1,0:T(8,128)(2,1)}), bf16[1536,12288]{1,0:T(8,128)(2,1)}) %all-gather.2.cloned.1.call-update) | async-done | bytes 37748752 | tf_op jit(solution)/shard_map/all_gather | solution.py:9
  226.3 78.8 %fusion = f32[1536,1792]{1,0:T(8,128)} fusion(bf16[1536,12288]{1,0:T(8,128)(2,1)} %all-gather.2.cloned.1.call-done, bf16[12288,1792]{1,0:T(8,128)(2,1)} %param.5), kind=kOutput, calls=%fused_computation.2 | convolution fusion | flops 67645734912 | bytes 92798976 | tf_op jit(solution)/shard_map/dot_general | solution.py:10
  305.1 81.0 %multiply_convert_fusion = bf16[1536,1792]{1,0:T(8,128)(2,1)} fusion(f32[1536,1792]{1,0:T(8,128)} %fusion, bf16[1536,12288]{1,0:T(8,128)(2,1)} %all-gather.2.cloned.1.call-done, bf16[12288,1792]{1,0:T(8,128)(2,1)} %param.6), kind=kOutput, calls=%fused_computation.1 | convolution fusion | flops 67662249984 | bytes 98304000 | tf_op jit(solution)/shard_map/dot_general | solution.py:11
  386.2 76.4 %convolution_convert_fusion = bf16[1536,12288]{1,0:T(8,128)(2,1)} fusion(bf16[1536,1792]{1,0:T(8,128)(2,1)} %multiply_convert_fusion, bf16[1792,12288]{1,0:T(8,128)(2,1)} %param.7), kind=kOutput, calls=%fused_computation | convolution fusion | flops 67664609280 | bytes 87293952 | tf_op jit(solution)/shard_map/dot_general | solution.py:13
  462.6 0.1 reduce-scatter.2.cloned.1.call-update
  462.7 210.2 %reduce-scatter.2.cloned.1.call-done = bf16[96,12288]{1,0:T(8,128)(2,1)} async-done(((bf16[1536,12288]{1,0:T(8,128)(2,1)}), bf16[96,12288]{1,0:T(8,128)(2,1)}) %reduce-scatter.2.cloned.1.call-update) | async-done | bytes 2359312 | tf_op jit(solution)/shard_map/reduce_scatter | solution.py:14
Async XLA Ops:
  6.5 219.8 %all-gather.2.cloned.1.call-start = ((), (), s32[]{:S(2)}) async-start(), calls=%async_computation.1 | async-start | bytes 40108032 | tf_op jit(solution)/shard_map/all_gather | solution.py:9
  7.3 665.6 %reduce-scatter.2.cloned.1.call-start = ((), (), s32[]{:S(2)}) async-start(), calls=%async_computation.2 | async-start | bytes 40108032 | tf_op jit(solution)/shard_map/reduce_scatter | solution.py:14
Sparse Core Ops, SparseCore 0:
  9.3 216.9 all-gather.1
  462.8 210.0 reduce-scatter.1
where the time goes:
time: 680 us
  waiting for transfers between devices  430 us (63%)
  matrix products  236 us (35%)
  between operations  13.4 us (2%)
    all_gather x1, waiting for transfers between devices, step(): rows = lax.all_gather(x, 'tp', axis=0, tiled=True)  219 us
    reduce_scatter x1, waiting for transfers between devices, step(): return lax.psum_scatter(term, 'tp', scatter_dimension=0, tiled=True)  210 us
    dot_general x1, matrix products, step(): up = jnp.dot(rows, w_up, preferred_element_type=jnp.float32)  81 us
    dot_general x1, matrix products, step(): gate = jnp.dot(rows, w_gate, preferred_element_type=jnp.float32)  78.8 us
    dot_general x1, matrix products, step(): jnp.dot(hidden, w_down, preferred_element_type=jnp.float32)  76.4 us
  transfers between devices with their start and end apart: 2, of which 2 were waited for; matrix products, arithmetic and copies ran while one was open for 0% of the time, Pallas kernels for 0%

commit v1 on v0

v1 whole, which is shorter than its diff:
```python
import functools
import math

import jax
import jax.numpy as jnp
from jax import lax
from jax.experimental import pallas as pl
from jax.experimental.pallas import tpu as pltpu
from jax.sharding import PartitionSpec as P

COMPUTE = True
COMM = True

BF16, F32 = jnp.bfloat16, jnp.float32
RINGS = 4
ROWS = 8
BLOCKS = 4
K_TILES = 24
N_TILES = 12
WEIGHT_SLOTS = 3
HOP_SLOTS = 4


def kernel(
    n, x_ref, wg_ref, wu_ref, wd_ref, y_ref, xg_ref, t_ref,
    wg_buf, wu_buf, wd_buf, x_buf, acc_g, acc_u, hid, t_buf, term_buf, send_buf, sum_buf,
    wgu_sem, wd_sem, x_sem, t_sem, term_sem, y_sem,
    ag_send, ag_recv, rs_send, rs_recv, credit,
):
    m, d = x_ref.shape
    part = m // RINGS
    subs = part // ROWS
    per_hop = RINGS * subs
    block = n * m // BLOCKS
    kt, nt = d // K_TILES, d // N_TILES
    side = math.isqrt(n)

    me = lax.axis_index("tp")
    px, py = me // side, me % side
    diagonal = (px + py) % side

    def by_x(t):
        a, b = t // side, t % side
        return a * side + (b - a + side) % side

    def by_y(t):
        a, b = t // side, t % side
        return (b - a + side) % side * side + a

    at_x, at_y = px * side + diagonal, py * side + diagonal
    ahead_x, behind_x = by_x((at_x + 1) % n), by_x((at_x + n - 1) % n)
    ahead_y, behind_y = by_y((at_y + 1) % n), by_y((at_y + n - 1) % n)
    target = (ahead_x, behind_x, ahead_y, behind_y)
    origin = (behind_x, ahead_x, behind_y, ahead_y)

    def rows_of(s, r, j):
        return pl.ds(pl.multiple_of(((s * RINGS + r) * subs + j) * ROWS, ROWS), ROWS)

    def ag_copy(s, r, j, src):
        return pltpu.make_async_remote_copy(
            src_ref=src,
            dst_ref=xg_ref.at[rows_of(s + 1, r, j), :],
            send_sem=ag_send.at[r * subs + j],
            recv_sem=ag_recv.at[s * per_hop + r * subs + j],
            device_id={"tp": target[r]},
            device_id_type=pl.DeviceIdType.MESH,
        )

    def ag_first():
        for j in range(subs):
            for r in range(RINGS):
                ag_copy(0, r, j, x_ref.at[rows_of(0, r, j), :]).start()

    def ag_service(q):
        s, j = q // subs + 1, q % subs
        for r in range(RINGS):
            ag_copy(s - 1, r, j, xg_ref.at[rows_of(s, r, j), :]).wait_recv()

            @pl.when(s < n - 1)
            def _():
                copy = ag_copy(s, r, j, xg_ref.at[rows_of(s, r, j), :])
                copy.wait_send()
                copy.start()

    def ag_last():
        for j in range(subs):
            for r in range(RINGS):
                ag_copy(0, r, j, x_ref.at[rows_of(0, r, j), :]).wait_send()

    def term_copy(p, r):
        h, j = p // subs + 1, p % subs
        return pltpu.make_async_copy(
            t_ref.at[rows_of(h % n, r, j), :], term_buf.at[p % 2, r], term_sem.at[p % 2, r]
        )

    def term_start(p):
        for r in range(RINGS):
            term_copy(p, r).start()

    def rs_copy(h, r, j):
        return pltpu.make_async_remote_copy(
            src_ref=send_buf.at[r * subs + j],
            dst_ref=sum_buf.at[(h + 1) % HOP_SLOTS * per_hop + r * subs + j],
            send_sem=rs_send.at[r * subs + j],
            recv_sem=rs_recv.at[(h + 1) % HOP_SLOTS * per_hop + r * subs + j],
            device_id={"tp": target[r]},
            device_id_type=pl.DeviceIdType.MESH,
        )

    def rs_add(p, r, first):
        h, j = p // subs + 1, p % subs
        term_copy(p, r).wait()
        total = term_buf[p % 2, r]
        if not first:
            rs_copy(h - 1, r, j).wait_recv()
            rs_copy(h - 1, r, j).wait_send()
            total += sum_buf[h % HOP_SLOTS * per_hop + r * subs + j].astype(F32)
        send_buf[r * subs + j] = total.astype(BF16)
        if not first:

            @pl.when(h + HOP_SLOTS <= n)
            def _():
                pl.semaphore_signal(
                    credit.at[r * subs + j],
                    inc=1,
                    device_id={"tp": origin[r]},
                    device_id_type=pl.DeviceIdType.MESH,
                )

    def rs_service(p, first):
        h, j = p // subs + 1, p % subs
        for r in range(RINGS):
            rs_add(p, r, first)
        for r in range(RINGS):
            if not first:

                @pl.when(h > HOP_SLOTS)
                def _():
                    pl.semaphore_wait(credit.at[r * subs + j], 1)

            rs_copy(h, r, j).start()
        term_start(p + 1)

    def y_copy(r, j):
        return pltpu.make_async_copy(
            send_buf.at[r * subs + j], y_ref.at[rows_of(0, r, j), :], y_sem.at[r * subs + j]
        )

    def gu_copies(g):
        k = pl.ds(pl.multiple_of(g % K_TILES * kt, kt), kt)
        slot = g % WEIGHT_SLOTS
        return (
            pltpu.make_async_copy(wg_ref.at[k, :], wg_buf.at[slot], wgu_sem.at[slot, 0]),
            pltpu.make_async_copy(wu_ref.at[k, :], wu_buf.at[slot], wgu_sem.at[slot, 1]),
        )

    def wd_copy(e):
        cols = pl.ds(pl.multiple_of(e % N_TILES * nt, nt), nt)
        slot = e % WEIGHT_SLOTS
        return pltpu.make_async_copy(wd_ref.at[:, cols], wd_buf.at[slot], wd_sem.at[slot])

    def x_start(b, i):
        k = pl.ds(pl.multiple_of(i * kt, kt), kt)

        @pl.when(b == 0)
        def _():
            pltpu.make_async_copy(
                x_ref.at[:, k], x_buf.at[i % 2, pl.ds(0, m), :], x_sem.at[i % 2]
            ).start()
            pltpu.make_async_copy(
                xg_ref.at[pl.ds(m, block - m), k], x_buf.at[i % 2, pl.ds(m, block - m), :], x_sem.at[i % 2]
            ).start()

        @pl.when(b > 0)
        def _():
            x_copy(b, i).start()

    def x_copy(b, i):
        k = pl.ds(pl.multiple_of(i * kt, kt), kt)
        return pltpu.make_async_copy(
            xg_ref.at[pl.ds(pl.multiple_of(b * block, block), block), k], x_buf.at[i % 2], x_sem.at[i % 2]
        )

    def t_copy(b, i):
        rows = pl.ds(pl.multiple_of(b * block, block), block)
        cols = pl.ds(pl.multiple_of(i * nt, nt), nt)
        return pltpu.make_async_copy(t_buf.at[i % 2], t_ref.at[rows, cols], t_sem.at[i % 2])

    def t_drain(b):
        t_copy(b, N_TILES - 2).wait()
        t_copy(b, N_TILES - 1).wait()

    f = wg_ref.shape[1]
    step_n = 256

    def gate_up(b, i):
        g = b * K_TILES + i
        slot = g % WEIGHT_SLOTS

        @pl.when(i == 0)
        def _():
            @pl.when(b > 0)
            def _():
                t_drain(b - 1)

            acc_g[...] = jnp.zeros_like(acc_g)
            acc_u[...] = jnp.zeros_like(acc_u)

        for copy in gu_copies(g):
            copy.wait()

        @pl.when(g + WEIGHT_SLOTS - 1 < BLOCKS * K_TILES)
        def _():
            for copy in gu_copies(g + WEIGHT_SLOTS - 1):
                copy.start()

        x_copy(b, i).wait()

        @pl.when(i + 1 < K_TILES)
        def _():
            x_start(b, i + 1)

        if COMPUTE:
            xt = x_buf[i % 2]
            for c in range(0, f, step_n):
                acc_g[:, c : c + step_n] += jnp.dot(xt, wg_buf[slot, :, c : c + step_n], preferred_element_type=F32)
                acc_u[:, c : c + step_n] += jnp.dot(xt, wu_buf[slot, :, c : c + step_n], preferred_element_type=F32)

        @pl.when(i == K_TILES - 1)
        def _():
            def chunk(c, _):
                rows = pl.ds(pl.multiple_of(c * 16, 16), 16)
                hid[rows, :] = (jax.nn.silu(acc_g[rows, :]) * acc_u[rows, :]).astype(BF16)
                return 0

            lax.fori_loop(0, block // 16, chunk, 0)

    def down(b, i):
        e = b * N_TILES + i
        slot = e % WEIGHT_SLOTS
        wd_copy(e).wait()

        @pl.when(e + WEIGHT_SLOTS - 1 < BLOCKS * N_TILES)
        def _():
            wd_copy(e + WEIGHT_SLOTS - 1).start()

        @pl.when(i >= 2)
        def _():
            t_copy(b, i - 2).wait()

        if COMPUTE:
            for c in range(0, nt, step_n):
                t_buf[i % 2, :, c : c + step_n] = jnp.dot(
                    hid[...], wd_buf[slot, :, c : c + step_n], preferred_element_type=F32
                )
        t_copy(b, i).start()

        @pl.when((i == N_TILES - 1) & (b < BLOCKS - 1))
        def _():
            x_start(b + 1, 0)

    barrier = pltpu.get_barrier_semaphore()
    for r in range(RINGS):
        pl.semaphore_signal(barrier, inc=1, device_id={"tp": target[r]}, device_id_type=pl.DeviceIdType.MESH)
    pl.semaphore_wait(barrier, RINGS)

    if COMM:
        ag_first()
    for e in range(WEIGHT_SLOTS - 1):
        for copy in gu_copies(e):
            copy.start()
        wd_copy(e).start()

    ticks = K_TILES + N_TILES
    lead = (n // BLOCKS - 1) * subs
    ag_pieces = (n - 1) * subs
    ag_num, ag_den = 2, 5
    rs_at = -((lead - ag_pieces) * ag_den // ag_num) + 2
    rs_num, rs_den = 4, 7

    if COMM:
        lax.fori_loop(0, lead, lambda q, _: (ag_service(q), 0)[1], 0)
    x_start(0, 0)

    def tick(t, _):
        b, i = t // ticks, t % ticks

        @pl.when(i < K_TILES)
        def _():
            gate_up(b, i)

        @pl.when(i >= K_TILES)
        def _():
            down(b, i - K_TILES)

        if COMM:
            q = lead + t * ag_num // ag_den

            @pl.when((q < ag_pieces) & (t * ag_num % ag_den < ag_num))
            def _():
                ag_service(q)

            @pl.when(t == rs_at - 1)
            def _():
                term_start(0)

            u = t - rs_at
            p = u * rs_num // rs_den

            @pl.when((u >= 0) & (u * rs_num % rs_den < rs_num))
            def _():
                @pl.when(p < subs)
                def _():
                    rs_service(p, True)

                @pl.when(p >= subs)
                def _():
                    rs_service(p, False)

        return 0

    total = BLOCKS * ticks
    lax.fori_loop(0, total, tick, 0)
    t_drain(BLOCKS - 1)
    if COMM:
        ag_last()
        p0 = ((total - 1 - rs_at) * rs_num) // rs_den + 1
        lax.fori_loop(p0, (n - 1) * subs, lambda p, _: (rs_service(p, False), 0)[1], 0)
        for j in range(subs):
            p = (n - 1) * subs + j
            for r in range(RINGS):
                rs_add(p, r, False)
                y_copy(r, j).start()
            if j + 1 < subs:
                term_start(p + 1)
        for j in range(subs):
            for r in range(RINGS):
                y_copy(r, j).wait()


def solution(mesh):
    n = mesh.shape["tp"]

    def step(x, w_gate, w_up, w_down):
        m, d = x.shape
        f = w_gate.shape[1]
        block = n * m // BLOCKS
        kt, nt = d // K_TILES, d // N_TILES
        subs = m // RINGS // ROWS
        per_hop = RINGS * subs
        dma = pltpu.SemaphoreType.DMA
        hbm = pl.BlockSpec(memory_space=pl.ANY)
        y, _, _ = pl.pallas_call(
            functools.partial(kernel, n),
            out_shape=(
                jax.ShapeDtypeStruct((m, d), BF16),
                jax.ShapeDtypeStruct((n * m, d), BF16),
                jax.ShapeDtypeStruct((n * m, d), F32),
            ),
            in_specs=[hbm] * 4,
            out_specs=(hbm,) * 3,
            scratch_shapes=[
                pltpu.VMEM((WEIGHT_SLOTS, kt, f), BF16),
                pltpu.VMEM((WEIGHT_SLOTS, kt, f), BF16),
                pltpu.VMEM((WEIGHT_SLOTS, f, nt), BF16),
                pltpu.VMEM((2, block, kt), BF16),
                pltpu.VMEM((block, f), F32),
                pltpu.VMEM((block, f), F32),
                pltpu.VMEM((block, f), BF16),
                pltpu.VMEM((2, block, nt), F32),
                pltpu.VMEM((2, RINGS, ROWS, d), F32),
                pltpu.VMEM((per_hop, ROWS, d), BF16),
                pltpu.VMEM((HOP_SLOTS * per_hop, ROWS, d), BF16),
                dma((WEIGHT_SLOTS, 2)),
                dma((WEIGHT_SLOTS,)),
                dma((2,)),
                dma((2,)),
                dma((2, RINGS)),
                dma((per_hop,)),
                dma((per_hop,)),
                dma(((n - 1) * per_hop,)),
                dma((per_hop,)),
                dma((HOP_SLOTS * per_hop,)),
                pltpu.SemaphoreType.REGULAR((per_hop,)),
            ],
            compiler_params=pltpu.CompilerParams(
                collective_id=0, has_side_effects=True, vmem_limit_bytes=64 * 1000 * 1000
            ),
        )(x, w_gate, w_up, w_down)
        return y

    return jax.shard_map(
        step,
        mesh=mesh,
        in_specs=(P(("dp", "tp"), None), P(None, "tp"), P(None, "tp"), P("tp", None)),
        out_specs=P(("dp", "tp"), None),
        check_vma=False,
    )
```

time: 680 us -> 425 us (0.62)
  waiting for transfers between devices: 430 us -> 0 us
  Pallas kernels: 0 us -> 421 us
  matrix products: 236 us -> 0 us
  between operations: 13.4 us -> 0.01 us
    pallas_call x0 -> x1, Pallas kernels: none -> 421 us  [step(): pl.pallas_call(functools.partial(kernel, n), out_shape=(jax.ShapeDtypeStr...]
    dot_general x3 -> x0, matrix products: 236 us -> none  [the longest x1 81 us: step(): up = jnp.dot(rows, w_up, preferred_element_type=jnp.float32)]
    all_gather x1 -> x0, waiting for transfers between devices: 219 us -> none  [step(): rows = lax.all_gather(x, 'tp', axis=0, tiled=True)]
    reduce_scatter x1 -> x0, waiting for transfers between devices: 210 us -> none  [step(): return lax.psum_scatter(term, 'tp', scatter_dimension=0, tiled=True)]
  transfers between devices with their start and end apart: 2 -> 0, of which waited for: 2 -> 0; matrix products, arithmetic and copies ran while one was open for 0% -> 0% of each run, Pallas kernels for 0% -> 0%
where the time goes in v1:
time: 425 us; the launch traced here: 424 us
  Pallas kernels  421 us (99%)
    pallas_call x1, Pallas kernels, step(): pl.pallas_call(functools.partial(kernel, n), out_shape=(jax.ShapeDtypeStr...  421 us

profile of v1, /device:TPU:97, one launch (start us, length us, event | category | flops | bytes accessed | tf_op | source)
XLA Modules:
  0.0 423.9 jit_solution(9717971749588719932)
XLA Ops:
  0.0 420.6 %shard_map.46 = (bf16[96,12288]{1,0:T(8,128)(2,1)}, bf16[1536,12288]{1,0:T(8,128)(2,1)}, f32[1536,12288]{1,0:T(8,128)}) custom-call(bf16[96,12288]{1,0:T(8,128)(2,1)} %x_ref.1, bf16[12288,1792]{1,0:T(8,128)(2,1)} %wg_ref.1, bf16[12288,1792]{1,0:T(8,128)(2,1)} %wu_ref.1, bf16[1792,12288]{1,0:T(8,128)(2,1)} %wd_ref.1), custom_call_target="tpu_custom_call" | custom-call | tf_op jit(solution)/shard_map/pallas_call | solution.py:353
  420.6 3.2 copy.6

commit v2 on v1

--- a/solution.py
+++ b/solution.py
@@ -18,6 +18,8 @@
 K_TILES = 24
 N_TILES = 12
 WEIGHT_SLOTS = 3
+X_SLOTS = 3
+GATHER_TICKS = 77
 HOP_SLOTS = 4
 
 
@@ -74,18 +76,16 @@
     def ag_service(q):
         s, j = q // subs + 1, q % subs
         for r in range(RINGS):
+            copy = ag_copy(s, r, j, xg_ref.at[rows_of(s, r, j), :])
             ag_copy(s - 1, r, j, xg_ref.at[rows_of(s, r, j), :]).wait_recv()
-
-            @pl.when(s < n - 1)
-            def _():
-                copy = ag_copy(s, r, j, xg_ref.at[rows_of(s, r, j), :])
-                copy.wait_send()
-                copy.start()
-
-    def ag_last():
-        for j in range(subs):
-            for r in range(RINGS):
-                ag_copy(0, r, j, x_ref.at[rows_of(0, r, j), :]).wait_send()
+            copy.wait_send()
+            copy.start()
+
+    def ag_last(j):
+        for r in range(RINGS):
+            copy = ag_copy(n - 2, r, j, xg_ref.at[rows_of(n - 2, r, j), :])
+            copy.wait_send()
+            copy.wait_recv()
 
     def term_copy(p, r):
         h, j = p // subs + 1, p % subs
@@ -165,10 +165,10 @@
         @pl.when(b == 0)
         def _():
             pltpu.make_async_copy(
-                x_ref.at[:, k], x_buf.at[i % 2, pl.ds(0, m), :], x_sem.at[i % 2]
+                x_ref.at[:, k], x_buf.at[i % X_SLOTS, pl.ds(0, m), :], x_sem.at[i % X_SLOTS]
             ).start()
             pltpu.make_async_copy(
-                xg_ref.at[pl.ds(m, block - m), k], x_buf.at[i % 2, pl.ds(m, block - m), :], x_sem.at[i % 2]
+                xg_ref.at[pl.ds(m, block - m), k], x_buf.at[i % X_SLOTS, pl.ds(m, block - m), :], x_sem.at[i % X_SLOTS]
             ).start()
 
         @pl.when(b > 0)
@@ -178,7 +178,7 @@
     def x_copy(b, i):
         k = pl.ds(pl.multiple_of(i * kt, kt), kt)
         return pltpu.make_async_copy(
-            xg_ref.at[pl.ds(pl.multiple_of(b * block, block), block), k], x_buf.at[i % 2], x_sem.at[i % 2]
+            xg_ref.at[pl.ds(pl.multiple_of(b * block, block), block), k], x_buf.at[i % X_SLOTS], x_sem.at[i % X_SLOTS]
         )
 
     def t_copy(b, i):
@@ -206,22 +206,21 @@
             acc_g[...] = jnp.zeros_like(acc_g)
             acc_u[...] = jnp.zeros_like(acc_u)
 
+        @pl.when(i + X_SLOTS - 1 < K_TILES)
+        def _():
+            x_start(b, i + X_SLOTS - 1)
+
+        @pl.when(g + WEIGHT_SLOTS - 1 < BLOCKS * K_TILES)
+        def _():
+            for copy in gu_copies(g + WEIGHT_SLOTS - 1):
+                copy.start()
+
+        x_copy(b, i).wait()
         for copy in gu_copies(g):
             copy.wait()
 
-        @pl.when(g + WEIGHT_SLOTS - 1 < BLOCKS * K_TILES)
-        def _():
-            for copy in gu_copies(g + WEIGHT_SLOTS - 1):
-                copy.start()
-
-        x_copy(b, i).wait()
-
-        @pl.when(i + 1 < K_TILES)
-        def _():
-            x_start(b, i + 1)
-
         if COMPUTE:
-            xt = x_buf[i % 2]
+            xt = x_buf[i % X_SLOTS]
             for c in range(0, f, step_n):
                 acc_g[:, c : c + step_n] += jnp.dot(xt, wg_buf[slot, :, c : c + step_n], preferred_element_type=F32)
                 acc_u[:, c : c + step_n] += jnp.dot(xt, wu_buf[slot, :, c : c + step_n], preferred_element_type=F32)
@@ -255,9 +254,11 @@
                 )
         t_copy(b, i).start()
 
-        @pl.when((i == N_TILES - 1) & (b < BLOCKS - 1))
-        def _():
-            x_start(b + 1, 0)
+        ahead = i - (N_TILES - X_SLOTS + 1)
+
+        @pl.when((ahead >= 0) & (b < BLOCKS - 1))
+        def _():
+            x_start(b + 1, ahead)
 
     barrier = pltpu.get_barrier_semaphore()
     for r in range(RINGS):
@@ -272,15 +273,36 @@
         wd_copy(e).start()
 
     ticks = K_TILES + N_TILES
+    total = BLOCKS * ticks
     lead = (n // BLOCKS - 1) * subs
-    ag_pieces = (n - 1) * subs
-    ag_num, ag_den = 2, 5
-    rs_at = -((lead - ag_pieces) * ag_den // ag_num) + 2
-    rs_num, rs_den = 4, 7
+    forwards = (n - 2) * subs
+    last_terms = (n - n // BLOCKS - 1) * subs
+
+    def serve(z):
+        @pl.when(z < forwards)
+        def _():
+            ag_service(z)
+
+        @pl.when(z == forwards - 1)
+        def _():
+            term_start(0)
+
+        @pl.when((z >= forwards) & (z < forwards + subs))
+        def _():
+            rs_service(z - forwards, True)
+
+        @pl.when(z >= forwards + subs)
+        def _():
+            rs_service(z - forwards, False)
+
+        @pl.when((z >= forwards + subs) & (z < forwards + 2 * subs))
+        def _():
+            ag_last(z - forwards - subs)
 
     if COMM:
         lax.fori_loop(0, lead, lambda q, _: (ag_service(q), 0)[1], 0)
-    x_start(0, 0)
+    for i in range(X_SLOTS - 1):
+        x_start(0, i)
 
     def tick(t, _):
         b, i = t // ticks, t % ticks
@@ -294,38 +316,25 @@
             down(b, i - K_TILES)
 
         if COMM:
-            q = lead + t * ag_num // ag_den
-
-            @pl.when((q < ag_pieces) & (t * ag_num % ag_den < ag_num))
+            u = t * (forwards - lead)
+
+            @pl.when((t < GATHER_TICKS) & (u % GATHER_TICKS < forwards - lead))
             def _():
-                ag_service(q)
-
-            @pl.when(t == rs_at - 1)
+                serve(lead + u // GATHER_TICKS)
+
+            v = (t - GATHER_TICKS) * (last_terms - 1)
+            rest = total - GATHER_TICKS
+
+            @pl.when((t >= GATHER_TICKS) & (v % rest < last_terms - 1))
             def _():
-                term_start(0)
-
-            u = t - rs_at
-            p = u * rs_num // rs_den
-
-            @pl.when((u >= 0) & (u * rs_num % rs_den < rs_num))
-            def _():
-                @pl.when(p < subs)
-                def _():
-                    rs_service(p, True)
-
-                @pl.when(p >= subs)
-                def _():
-                    rs_service(p, False)
+                serve(forwards + v // rest)
 
         return 0
 
-    total = BLOCKS * ticks
     lax.fori_loop(0, total, tick, 0)
     t_drain(BLOCKS - 1)
     if COMM:
-        ag_last()
-        p0 = ((total - 1 - rs_at) * rs_num) // rs_den + 1
-        lax.fori_loop(p0, (n - 1) * subs, lambda p, _: (rs_service(p, False), 0)[1], 0)
+        lax.fori_loop(last_terms - 1, (n - 1) * subs, lambda p, _: (rs_service(p, False), 0)[1], 0)
         for j in range(subs):
             p = (n - 1) * subs + j
             for r in range(RINGS):
@@ -363,7 +372,7 @@
                 pltpu.VMEM((WEIGHT_SLOTS, kt, f), BF16),
                 pltpu.VMEM((WEIGHT_SLOTS, kt, f), BF16),
                 pltpu.VMEM((WEIGHT_SLOTS, f, nt), BF16),
-                pltpu.VMEM((2, block, kt), BF16),
+                pltpu.VMEM((X_SLOTS, block, kt), BF16),
                 pltpu.VMEM((block, f), F32),
                 pltpu.VMEM((block, f), F32),
                 pltpu.VMEM((block, f), BF16),
@@ -373,7 +382,7 @@
                 pltpu.VMEM((HOP_SLOTS * per_hop, ROWS, d), BF16),
                 dma((WEIGHT_SLOTS, 2)),
                 dma((WEIGHT_SLOTS,)),
-                dma((2,)),
+                dma((X_SLOTS,)),
                 dma((2,)),
                 dma((2, RINGS)),
                 dma((per_hop,)),

time: 425 us -> 395 us (0.929)
  Pallas kernels: 421 us -> 391 us
    pallas_call x1, Pallas kernels: 421 us -> 391 us  [step(): pl.pallas_call(functools.partial(kernel, n), out_shape=(jax.ShapeDtypeStr...]
where the time goes in v2:
time: 395 us; the launch traced here: 394 us
  Pallas kernels  391 us (99%)
    pallas_call x1, Pallas kernels, step(): pl.pallas_call(functools.partial(kernel, n), out_shape=(jax.ShapeDtypeStr...  391 us

profile of v2, /device:TPU:97, one launch (start us, length us, event | category | flops | bytes accessed | tf_op | source)
XLA Modules:
  0.0 394.3 jit_solution(1961611800011603491)
XLA Ops:
  0.0 391.1 %shard_map.46 = (bf16[96,12288]{1,0:T(8,128)(2,1)}, bf16[1536,12288]{1,0:T(8,128)(2,1)}, f32[1536,12288]{1,0:T(8,128)}) custom-call(bf16[96,12288]{1,0:T(8,128)(2,1)} %x_ref.1, bf16[12288,1792]{1,0:T(8,128)(2,1)} %wg_ref.1, bf16[12288,1792]{1,0:T(8,128)(2,1)} %wu_ref.1, bf16[1792,12288]{1,0:T(8,128)(2,1)} %wd_ref.1), custom_call_target="tpu_custom_call" | custom-call | tf_op jit(solution)/shard_map/pallas_call | solution.py:362
  391.1 3.2 copy.6

commit v3 on v2

--- a/solution.py
+++ b/solution.py
@@ -20,14 +20,14 @@
 WEIGHT_SLOTS = 3
 X_SLOTS = 3
 GATHER_TICKS = 77
-HOP_SLOTS = 4
+HOP_SLOTS = 3
 
 
 def kernel(
-    n, x_ref, wg_ref, wu_ref, wd_ref, y_ref, xg_ref, t_ref,
+    n, x_ref, wg_ref, wu_ref, wd_ref, sum_ref, own_ref, xg_ref, t_ref,
     wg_buf, wu_buf, wd_buf, x_buf, acc_g, acc_u, hid, t_buf, term_buf, send_buf, sum_buf,
-    wgu_sem, wd_sem, x_sem, t_sem, term_sem, y_sem,
-    ag_send, ag_recv, rs_send, rs_recv, credit,
+    wgu_sem, wd_sem, x_sem, t_sem, term_sem, own_sem,
+    ag_send, ag_recv, rs_send, rs_recv, last_recv, credit,
 ):
     m, d = x_ref.shape
     part = m // RINGS
@@ -103,6 +103,19 @@
             dst_ref=sum_buf.at[(h + 1) % HOP_SLOTS * per_hop + r * subs + j],
             send_sem=rs_send.at[r * subs + j],
             recv_sem=rs_recv.at[(h + 1) % HOP_SLOTS * per_hop + r * subs + j],
+            device_id={"tp": target[r]},
+            device_id_type=pl.DeviceIdType.MESH,
+        )
+
+    def own_copy():
+        return pltpu.make_async_copy(t_ref.at[pl.ds(0, m), :], own_ref, own_sem)
+
+    def last_copy(r, j):
+        return pltpu.make_async_remote_copy(
+            src_ref=send_buf.at[r * subs + j],
+            dst_ref=sum_ref.at[rows_of(0, r, j), :],
+            send_sem=rs_send.at[r * subs + j],
+            recv_sem=last_recv.at[r * subs + j],
             device_id={"tp": target[r]},
             device_id_type=pl.DeviceIdType.MESH,
         )
@@ -118,7 +131,7 @@
         send_buf[r * subs + j] = total.astype(BF16)
         if not first:
 
-            @pl.when(h + HOP_SLOTS <= n)
+            @pl.when(h + HOP_SLOTS < n)
             def _():
                 pl.semaphore_signal(
                     credit.at[r * subs + j],
@@ -127,24 +140,25 @@
                     device_id_type=pl.DeviceIdType.MESH,
                 )
 
-    def rs_service(p, first):
+    def rs_service(p, first, last=False):
         h, j = p // subs + 1, p % subs
         for r in range(RINGS):
             rs_add(p, r, first)
         for r in range(RINGS):
-            if not first:
+            if not first and not last:
 
                 @pl.when(h > HOP_SLOTS)
                 def _():
                     pl.semaphore_wait(credit.at[r * subs + j], 1)
 
-            rs_copy(h, r, j).start()
-        term_start(p + 1)
-
-    def y_copy(r, j):
-        return pltpu.make_async_copy(
-            send_buf.at[r * subs + j], y_ref.at[rows_of(0, r, j), :], y_sem.at[r * subs + j]
-        )
+            if last:
+                last_copy(r, j).start()
+            else:
+                rs_copy(h, r, j).start()
+        if not last:
+            term_start(p + 1)
+        elif p + 1 < (n - 1) * subs:
+            term_start(p + 1)
 
     def gu_copies(g):
         k = pl.ds(pl.multiple_of(g % K_TILES * kt, kt), kt)
@@ -286,6 +300,7 @@
         @pl.when(z == forwards - 1)
         def _():
             term_start(0)
+            own_copy().start()
 
         @pl.when((z >= forwards) & (z < forwards + subs))
         def _():
@@ -334,17 +349,14 @@
     lax.fori_loop(0, total, tick, 0)
     t_drain(BLOCKS - 1)
     if COMM:
-        lax.fori_loop(last_terms - 1, (n - 1) * subs, lambda p, _: (rs_service(p, False), 0)[1], 0)
+        lax.fori_loop(last_terms - 1, (n - 2) * subs, lambda p, _: (rs_service(p, False), 0)[1], 0)
         for j in range(subs):
-            p = (n - 1) * subs + j
-            for r in range(RINGS):
-                rs_add(p, r, False)
-                y_copy(r, j).start()
-            if j + 1 < subs:
-                term_start(p + 1)
+            rs_service((n - 2) * subs + j, False, True)
         for j in range(subs):
             for r in range(RINGS):
-                y_copy(r, j).wait()
+                last_copy(r, j).wait_recv()
+                last_copy(r, j).wait_send()
+        own_copy().wait()
 
 
 def solution(mesh):
@@ -359,15 +371,16 @@
         per_hop = RINGS * subs
         dma = pltpu.SemaphoreType.DMA
         hbm = pl.BlockSpec(memory_space=pl.ANY)
-        y, _, _ = pl.pallas_call(
+        sums, own, _, _ = pl.pallas_call(
             functools.partial(kernel, n),
             out_shape=(
                 jax.ShapeDtypeStruct((m, d), BF16),
+                jax.ShapeDtypeStruct((m, d), F32),
                 jax.ShapeDtypeStruct((n * m, d), BF16),
                 jax.ShapeDtypeStruct((n * m, d), F32),
             ),
             in_specs=[hbm] * 4,
-            out_specs=(hbm,) * 3,
+            out_specs=(hbm,) * 4,
             scratch_shapes=[
                 pltpu.VMEM((WEIGHT_SLOTS, kt, f), BF16),
                 pltpu.VMEM((WEIGHT_SLOTS, kt, f), BF16),
@@ -385,18 +398,19 @@
                 dma((X_SLOTS,)),
                 dma((2,)),
                 dma((2, RINGS)),
-                dma((per_hop,)),
+                dma(()),
                 dma((per_hop,)),
                 dma(((n - 1) * per_hop,)),
                 dma((per_hop,)),
                 dma((HOP_SLOTS * per_hop,)),
+                dma((per_hop,)),
                 pltpu.SemaphoreType.REGULAR((per_hop,)),
             ],
             compiler_params=pltpu.CompilerParams(
-                collective_id=0, has_side_effects=True, vmem_limit_bytes=64 * 1000 * 1000
+                collective_id=0, has_side_effects=True, vmem_limit_bytes=47_000_000
             ),
-        )(x, w_gate, w_up, w_down)
-        return y
+        )(pltpu.with_memory_space_constraint(x, pltpu.HBM), w_gate, w_up, w_down)
+        return (sums.astype(F32) + own).astype(BF16)
 
     return jax.shard_map(
         step,

time: 395 us -> 392 us (level)
  no operation moved by 1% of the time
where the time goes in v3:
time: 392 us
  Pallas kernels  390 us (99%)
    pallas_call x1, Pallas kernels, step(): pl.pallas_call(functools.partial(kernel, n), out_shape=(jax.ShapeDtypeStr...  390 us

profile of v3, /device:TPU:97, one launch (start us, length us, event | category | flops | bytes accessed | tf_op | source)
XLA Modules:
  0.0 391.9 jit_solution(801827810959154981)
XLA Ops:
  0.0 390.0 %shard_map.46 = (bf16[96,12288]{1,0:T(8,128)(2,1)S(1)}, f32[96,12288]{1,0:T(8,128)S(1)}, bf16[1536,12288]{1,0:T(8,128)(2,1)}, f32[1536,12288]{1,0:T(8,128)}) custom-call(bf16[96,12288]{1,0:T(8,128)(2,1)} %x_ref.1, bf16[12288,1792]{1,0:T(8,128)(2,1)} %wg_ref.1, bf16[12288,1792]{1,0:T(8,128)(2,1)} %wu_ref.1, bf16[1792,12288]{1,0:T(8,128)(2,1)} %wd_ref.1), custom_call_target="tpu_custom_call" | custom-call | tf_op jit(solution)/shard_map/pallas_call | solution.py:374
  390.0 1.9 add_convert_fusion
